TPU v7x, 32 devices: a whole 2x2x4 slice. The times are simulated.
32 devices in a mesh: seq: 8 (over z, x), fsdp: 4 (over y, core).
Axes of the slice: x: 2, y: 2, z: 4, core: 2. Of those that a mesh axis runs over, the one named last changes fastest.
Arguments:
- tokens: bfloat16 [4, 1024, 2048], P('fsdp', 'seq'), may hold values from -6 to 6
- cotangent: bfloat16 [4, 1024, 2048], P('fsdp', 'seq'), may hold values from -6 to 6
- routes: int32 [4, 1024, 8], P('fsdp', 'seq'), may hold values from 0 to 63, all different within a row; in each aligned block of 128 rows (0 to 127, 128 to 255, ..., all dimensions but the last counted through in order) at most 32 rows name the same one
- norm1_gain: bfloat16 [2048], P(('seq', 'fsdp')), may hold values from 0.099609375 to 1.8984375
- query_weight: bfloat16 [2048, 2048], P(('seq', 'fsdp')), may hold values from -0.125 to 0.125
- key_weight: bfloat16 [2048, 2048], P(('seq', 'fsdp')), may hold values from -0.125 to 0.125
- value_weight: bfloat16 [2048, 2048], P(('seq', 'fsdp')), may hold values from -0.125 to 0.125
- output_weight: bfloat16 [2048, 2048], P(('seq', 'fsdp')), may hold values from -2 to 2
- norm2_gain: bfloat16 [2048], P(('seq', 'fsdp')), may hold values from 0.099609375 to 1.8984375
- router_weight: bfloat16 [2048, 64], P(('seq', 'fsdp')), may hold values from -0.125 to 0.125
- expert_gate: bfloat16 [128, 2048, 512], P(('seq', 'fsdp')), may hold values from -0.125 to 0.125
- expert_up: bfloat16 [128, 2048, 512], P(('seq', 'fsdp')), may hold values from -0.125 to 0.125
- expert_down: bfloat16 [128, 512, 2048], P(('seq', 'fsdp')), may hold values from -0.75 to 0.75
Outputs:
- block_out: bfloat16 [4, 1024, 2048], P('fsdp', 'seq')
- input_grad: float32 [4, 1024, 2048], P('fsdp', 'seq')
- norm1_gain_grad: float32 [2048], P(('seq', 'fsdp'))
- query_weight_grad: float32 [2048, 2048], P(('seq', 'fsdp'))
- key_weight_grad: float32 [2048, 2048], P(('seq', 'fsdp'))
- value_weight_grad: float32 [2048, 2048], P(('seq', 'fsdp'))
- output_weight_grad: float32 [2048, 2048], P(('seq', 'fsdp'))
- norm2_gain_grad: float32 [2048], P(('seq', 'fsdp'))
- router_weight_grad: float32 [2048, 64], P(('seq', 'fsdp'))
- expert_gate_grad: float32 [128, 2048, 512], P(('seq', 'fsdp'))
- expert_up_grad: float32 [128, 2048, 512], P(('seq', 'fsdp'))
- expert_down_grad: float32 [128, 512, 2048], P(('seq', 'fsdp'))
Inputs may be any that keep to these rules, and one draw needn't show every extreme that they name: `routes`: each row names 8 different experts. Among the 128 rows of one device (aligned blocks of the flattened sequences) no expert is named more than 32 times, and in every draw some expert is named exactly 32 times in some block; every expert is named somewhere.
All inputs are finite; a program needn't handle non-finite values.
Results may differ from a plain program's by a relative error of at most 0.02.
Values may be sent and summed in bfloat16 or wider, within the bound.
A program may use at most 448 MiB of HBM per device.

v0:
```python
import jax
import jax.numpy as jnp
from jax import lax
from jax.sharding import PartitionSpec as P

H = 16
HD = 128
SPLIT = 2
AXES = ("seq", "fsdp")
epsilon = 1e-06
rope_base = 50000.0
bf16 = jnp.bfloat16
f32 = jnp.float32


def norm_rows(values, scales):
    mean_sq = jnp.mean(values * values, axis=-1, keepdims=True)
    return values * lax.rsqrt(mean_sq + epsilon) * scales


def rope_tables(positions, head_dim):
    half_dim = head_dim // 2
    frequency = rope_base ** (-(2.0 * jnp.arange(half_dim, dtype=f32)) / head_dim)
    angles = positions.astype(f32)[:, None] * frequency[None, :]
    return (jnp.cos(angles), jnp.sin(angles))


def rotate(values, cosine, sine_tab, inverse):
    half_dim = values.shape[-1] // 2
    low_half = values[..., :half_dim]
    high_half = values[..., half_dim:]
    cos_rows = cosine[:, None, :]
    sin_rows = -sine_tab[:, None, :] if inverse else sine_tab[:, None, :]
    return jnp.concatenate(
        [low_half * cos_rows - high_half * sin_rows, high_half * cos_rows + low_half * sin_rows],
        axis=-1,
    )


def route_weights(logits, chosen):
    expo = jnp.exp(logits)
    probability = expo / jnp.sum(expo, axis=-1, keepdims=True)
    experts = jnp.arange(logits.shape[1], dtype=jnp.int32)
    match = (chosen[:, :, None] == experts).astype(f32)
    picked = jnp.sum(match * probability[:, None, :], axis=-1)
    return picked / jnp.sum(picked, axis=-1, keepdims=True)


def mm(left, right):
    return jnp.dot(left, right, preferred_element_type=f32)


def mm_tn(left, right):
    return lax.dot_general(left, right, (((0,), (0,)), ((), ())), preferred_element_type=f32)


def mm_nt(left, right):
    return lax.dot_general(left, right, (((1,), (1,)), ((), ())), preferred_element_type=f32)


def ein(spec, *args):
    return jnp.einsum(spec, *args, preferred_element_type=f32)


def body(
    tokens,
    cotangent,
    routes,
    norm1_gain,
    query_weight,
    key_weight,
    value_weight,
    output_weight,
    norm2_gain,
    router_weight,
    expert_gate,
    expert_up,
    expert_down,
):
    n_seq = lax.axis_size("seq")
    n_fsdp = lax.axis_size("fsdp")
    n_dev = n_seq * n_fsdp
    seq_at = lax.axis_index("seq")
    dev_at = seq_at * n_fsdp + lax.axis_index("fsdp")
    tok_rows, width = (tokens.shape[1], tokens.shape[2])
    length = tok_rows * n_seq
    heads = H // n_seq
    cols = heads * HD
    shard = query_weight.shape[0]
    experts = router_weight.shape[1]
    top_k = routes.shape[2]
    capacity = tok_rows * top_k // experts * 2
    pieces = expert_gate.shape[0]
    n_loc = max(1, pieces // SPLIT)
    per_loc = pieces // n_loc
    first_expert = dev_at * pieces // SPLIT
    x_own = tokens[0]
    cot_own = cotangent[0]
    chosen = routes[0]
    routes_all = lax.all_gather(chosen, AXES, axis=0, tiled=True)
    x_seq = lax.all_gather(x_own, "seq", axis=0, tiled=True)
    small = jnp.concatenate(
        [
            router_weight,
            norm1_gain[:, None],
            norm2_gain[:, None],
            jnp.zeros((shard, 128 - experts - 2), bf16),
        ],
        axis=1,
    )
    blocks = jnp.concatenate(
        [
            query_weight.reshape(shard, n_seq, cols),
            key_weight.reshape(shard, n_seq, cols),
            value_weight.reshape(shard, n_seq, cols),
            jnp.broadcast_to(small[:, None, :], (shard, n_seq, 128)),
        ],
        axis=2,
    ).transpose(1, 0, 2)
    moved = lax.all_to_all(blocks, "seq", split_axis=0, concat_axis=0, tiled=True)
    packed = lax.all_gather(moved, "fsdp", axis=1).reshape(width, 3 * cols + 128)
    w_qkv = packed[:, : 3 * cols]
    router_full = packed[:, 3 * cols : 3 * cols + experts]
    gain_in = packed[:, 3 * cols + experts].astype(f32)
    gain_mid = packed[:, 3 * cols + experts + 1].astype(f32)
    out_full = lax.all_gather(output_weight, AXES, axis=0, tiled=True)
    out_rows = lax.dynamic_slice_in_dim(out_full, seq_at * cols, cols, 0)
    cot_all = lax.all_gather(cot_own, AXES, axis=0, tiled=True)
    cosine, sine_tab = rope_tables(jnp.arange(length, dtype=jnp.int32), HD)
    normed_in = norm_rows(x_seq.astype(f32), gain_in).astype(bf16)
    qkv = mm(normed_in, w_qkv)
    q = rotate(qkv[:, :cols].reshape(length, heads, HD), cosine, sine_tab, False).astype(bf16)
    k = rotate(qkv[:, cols : 2 * cols].reshape(length, heads, HD), cosine, sine_tab, False).astype(
        bf16
    )
    v = qkv[:, 2 * cols :].astype(bf16).reshape(length, heads, HD)
    scale = HD ** (-0.5)
    scores = ein("qhd,khd->hqk", q, k) * scale
    totals = jnp.log(jnp.sum(jnp.exp(scores), axis=-1))
    probs = jnp.exp(scores - totals[..., None])
    attn_heads = ein("hqk,khd->qhd", probs.astype(bf16), v).astype(bf16)
    attn_flat = attn_heads.reshape(length, cols)
    attn_rows = lax.all_to_all(attn_flat, "seq", split_axis=0, concat_axis=1, tiled=True)
    x_own32 = x_own.astype(f32)
    residual = x_own32 + mm(attn_rows, out_full)
    normed_mid = norm_rows(residual, gain_mid).astype(bf16)
    x_all = lax.all_gather(normed_mid, AXES, axis=0, tiled=True)
    logits_all = mm(x_all, router_full)
    w_all = route_weights(logits_all, routes_all)
    local = first_expert + jnp.arange(n_loc, dtype=jnp.int32)
    match = routes_all.reshape(n_dev, tok_rows, top_k)[:, None] == local[None, :, None, None]
    hit = jnp.any(match, axis=-1)
    w_hit = jnp.sum(jnp.where(match, w_all.reshape(n_dev, 1, tok_rows, top_k), 0.0), axis=-1)
    tri = (jnp.arange(tok_rows)[:, None] <= jnp.arange(tok_rows)[None, :]).astype(bf16)
    place = ein("bet,tu->beu", hit.astype(bf16), tri).astype(jnp.int32) - 1
    slots = jnp.arange(capacity, dtype=jnp.int32)
    pick = hit[:, :, None, :] & (place[:, :, None, :] == slots[None, None, :, None])
    one = pick.astype(bf16)
    w_slot = jnp.sum(jnp.where(pick, w_hit[:, :, None, :], 0.0), axis=-1)
    rows_of = lambda a: ein("best,btd->ebsd", one, a.reshape(n_dev, tok_rows, width)).reshape(
        n_loc, n_dev * capacity, width
    )
    rows_in = rows_of(x_all).astype(bf16)
    rows_cot = rows_of(cot_all)
    w_rows = w_slot.transpose(1, 0, 2).reshape(n_loc, n_dev * capacity, 1)
    rows_grad = (w_rows * rows_cot).astype(bf16)
    gate = expert_gate.reshape(n_loc, per_loc, width, -1)
    up = expert_up.reshape(n_loc, per_loc, width, -1)
    down = expert_down.reshape(n_loc, per_loc, -1, width)
    pre_gate = ein("erd,epdf->eprf", rows_in, gate)
    pre_up = ein("erd,epdf->eprf", rows_in, up)
    sig = jax.nn.sigmoid(pre_gate)
    active = pre_gate * sig
    hidden = (active * pre_up).astype(bf16)
    hidden_grad = ein("erd,epfd->eprf", rows_grad, down)
    gate_grad = (hidden_grad * pre_up * sig * (1.0 + pre_gate * (1.0 - sig))).astype(bf16)
    up_grad = (hidden_grad * active).astype(bf16)
    back = ein("eprf,epdf->erd", gate_grad, gate) + ein("eprf,epdf->erd", up_grad, up)
    out = ein("eprf,epfd->erd", hidden, down)
    w_back = jnp.sum(rows_cot * out, axis=-1)
    spread = (
        lambda a: ein("best,ebsd->btd", one, a.astype(bf16).reshape(n_loc, n_dev, capacity, width))
        .astype(bf16)
        .reshape(n_dev * tok_rows, width)
    )
    back_own = lax.psum_scatter(spread(back), AXES, scatter_dimension=0, tiled=True)
    w_tok = jnp.sum(
        jnp.where(pick, w_back.reshape(n_loc, n_dev, capacity).transpose(1, 0, 2)[..., None], 0.0),
        axis=2,
    )
    w_parts = lax.all_to_all(w_tok, AXES, split_axis=0, concat_axis=0, tiled=True)
    w_by_expert = w_parts.reshape(experts, n_dev * n_loc // experts, tok_rows).sum(axis=1)
    own_match = (chosen[:, :, None] == jnp.arange(experts, dtype=jnp.int32)).astype(f32)
    weight_grad = jnp.sum(own_match * w_by_expert.T[:, None, :], axis=-1)
    moe_own = lax.psum_scatter(spread(w_rows * out), AXES, scatter_dimension=0, tiled=True)
    block_out = (residual + moe_own.astype(f32)).astype(bf16)
    down_grad = ein("eprf,erd->epfd", hidden, rows_grad).reshape(expert_down.shape)
    gate_weight_grad = ein("erd,eprf->epdf", rows_in, gate_grad).reshape(expert_gate.shape)
    up_weight_grad = ein("erd,eprf->epdf", rows_in, up_grad).reshape(expert_up.shape)
    logits = mm(normed_mid, router_full)
    _, route_back = jax.vjp(lambda values: route_weights(values, chosen), logits)
    logit_grad = route_back(weight_grad)[0].astype(bf16)
    normed_total = back_own.astype(f32) + mm_nt(logit_grad, router_full)
    logit_all = lax.all_gather(logit_grad, AXES, axis=0, tiled=True)
    x_cols = lax.dynamic_slice_in_dim(x_all, dev_at * shard, shard, 1)
    grad_router = mm_tn(x_cols, logit_all)
    cot32 = cot_own.astype(f32)
    _, norm_back = jax.vjp(norm_rows, residual, gain_mid)
    resid_part, gain_two = norm_back(normed_total)
    resid_grad = cot32 + resid_part
    resid_seq = lax.all_gather(resid_grad.astype(bf16), "seq", axis=0, tiled=True)
    grad_out_rows = mm_tn(attn_flat, resid_seq)
    grad_output = lax.psum_scatter(grad_out_rows, "fsdp", scatter_dimension=0, tiled=True)
    attn_grad = mm_nt(resid_seq, out_rows).astype(bf16).reshape(length, heads, HD)
    delta = jnp.sum(attn_grad.astype(f32) * attn_heads.astype(f32), axis=-1)
    v_grad = ein("hqk,qhd->khd", probs.astype(bf16), attn_grad).astype(bf16)
    p_grad = ein("qhd,khd->hqk", attn_grad, v)
    s_grad = (probs * (p_grad - delta.T[:, :, None]) * scale).astype(bf16)
    q_grad = ein("hqk,khd->qhd", s_grad, k).astype(bf16)
    k_grad = ein("hqk,qhd->khd", s_grad, q).astype(bf16)
    q_rows = rotate(q_grad.astype(f32), cosine, sine_tab, True).astype(bf16)
    k_rows = rotate(k_grad.astype(f32), cosine, sine_tab, True).astype(bf16)
    d_qkv = jnp.concatenate([a.reshape(length, cols) for a in (q_rows, k_rows, v_grad)], axis=1)
    in_part = mm_nt(d_qkv, w_qkv).astype(bf16)
    normed_in_grad = lax.psum_scatter(in_part, "seq", scatter_dimension=0, tiled=True).astype(f32)
    _, norm_back_in = jax.vjp(norm_rows, x_own32, gain_in)
    input_part, gain_one = norm_back_in(normed_in_grad)
    input_grad = resid_grad + input_part
    grad_qkv = mm_tn(normed_in, d_qkv).reshape(n_seq, n_fsdp, shard, 3 * cols)
    grad_qkv = lax.psum_scatter(grad_qkv, "fsdp", scatter_dimension=1, tiled=False)
    grad_qkv = lax.all_to_all(grad_qkv, "seq", split_axis=0, concat_axis=0, tiled=True)
    grad_qkv = (
        grad_qkv.reshape(n_seq, shard, 3, cols).transpose(2, 1, 0, 3).reshape(3, shard, width)
    )
    gains = lax.psum_scatter(
        jnp.stack([gain_one, gain_two]).reshape(2, n_dev, shard),
        AXES,
        scatter_dimension=1,
        tiled=False,
    )
    return (
        block_out[None],
        input_grad[None],
        gains[0],
        grad_qkv[0],
        grad_qkv[1],
        grad_qkv[2],
        grad_output,
        gains[1],
        grad_router,
        gate_weight_grad,
        up_weight_grad,
        down_grad,
    )


def solution(mesh):
    rows3 = P("fsdp", "seq", None)
    flat = P(AXES)
    two = P(AXES, None)
    three = P(AXES, None, None)
    return jax.shard_map(
        body,
        mesh=mesh,
        in_specs=(rows3, rows3, rows3, flat, two, two, two, two, flat, two, three, three, three),
        out_specs=(rows3, rows3, flat, two, two, two, two, flat, two, three, three, three),
        check_vma=False,
    )
```

profile of v0, /device:TPU:0, one launch (start us, length us, event | category | flops | bytes accessed | tf_op | source)
XLA Modules:
  0.0 1324.9 jit_solution(16863959521056442889)
XLA Ops:
  12.9 30.4 %all_to_all.34 = bf16[8,64,896]{2,1,0:T(8,128)(2,1)S(1)} all-to-all(bf16[8,64,896]{2,1,0:T(8,128)(2,1)S(1)} %copy.233), channel_id=1, replica_groups=mesh['seq'=8,'fsdp'=4] {'seq'}, dimensions={0} | all-to-all | bytes 1835008 | tf_op jit(solution)/shard_map/all_to_all | solution.py:120
  46.9 3.1 fusion.80
  50.0 25.2 %all-gather.19.cloned.1.call-done = bf16[8,256,896]{2,0,1:T(8,128)(2,1)} async-done(((bf16[8,64,896]{2,0,1:T(8,128)(2,1)}), bf16[8,256,896]{2,0,1:T(8,128)(2,1)}) %all-gather.19.cloned.1.call-update) | async-done | bytes 3670032 | tf_op jit(solution)/shard_map/all_gather | solution.py:121
  80.2 69.8 %all-gather.17.cloned.1.call-done = bf16[1,1024,2048]{2,1,0:T(8,128)(2,1)} async-done(((bf16[1,128,2048]{2,1,0:T(8,128)(2,1)}), bf16[1,1024,2048]{2,1,0:T(8,128)(2,1)}) %all-gather.17.cloned.1.call-update) | async-done | bytes 4194320 | tf_op jit(solution)/shard_map/all_gather | solution.py:101
  150.0 3.1 fusion.5
  153.7 6.6 fusion.30
  171.2 3.4 subtract_convert_fusion.3
  174.6 9.4 fusion.8
  184.1 4.2 fusion.36
  189.1 28.2 %all_to_all.35 = bf16[8,128,256]{1,2,0:T(8,128)(2,1)S(1)} all-to-all(bf16[8,128,256]{1,2,0:T(8,128)(2,1)S(1)} %copy.241), channel_id=1, replica_groups=mesh['seq'=8,'fsdp'=4] {'seq'}, dimensions={0} | all-to-all | bytes 1048576 | tf_op jit(solution)/shard_map/all_to_all | solution.py:143
  217.3 14.1 %all-gather.11.cloned.1.call-done = bf16[2048,2048]{1,0:T(8,128)(2,1)} async-done(((bf16[64,2048]{1,0:T(8,128)(2,1)}), bf16[2048,2048]{1,0:T(8,128)(2,1)}) %all-gather.11.cloned.1.call-update) | async-done | bytes 8388624 | tf_op jit(solution)/shard_map/all_gather | solution.py:126
  231.4 4.8 multiply_reduce_fusion.3
  238.2 40.8 %all-gather.2 = s32[1,4096,8]{1,2,0:T(8,128)S(1)} all-gather(s32[1,128,8]{1,2,0:T(8,128)S(1)} %copy-done.24), channel_id=4, replica_groups=mesh['seq'=8,'fsdp'=4] {'seq','fsdp'}, dimensions={1}, use_global_device_ids=true | all-gather | bytes 135168 | tf_op jit(solution)/shard_map/all_gather | solution.py:100
  279.3 68.4 %all-gather.21.cloned.1.call-done = bf16[1,4096,2048]{2,1,0:T(8,128)(2,1)} async-done(((bf16[1,128,2048]{2,1,0:T(8,128)(2,1)}), bf16[1,4096,2048]{2,1,0:T(8,128)(2,1)}) %all-gather.21.cloned.1.call-update) | async-done | bytes 16777232 | tf_op jit(solution)/shard_map/all_gather | solution.py:128
  347.7 7.0 convolution_bitcast_fusion
  354.8 6.2 copy.247
  361.0 102.1 %all-gather.13.cloned.1.call-done = bf16[4096,2048]{1,0:T(8,128)(2,1)} async-done(((bf16[128,2048]{1,0:T(8,128)(2,1)}), bf16[4096,2048]{1,0:T(8,128)(2,1)}) %all-gather.13.cloned.1.call-update) | async-done | bytes 16777232 | tf_op jit(solution)/shard_map/all_gather | solution.py:147
  463.0 9.4 convert_bitcast_fusion
  472.4 8.3 copy.245
  480.7 15.8 %fusion.98 = f32[2,1024,2,512]{3,1,2,0:T(8,128)} fusion(bf16[2,1024,2048,1]{2,1,3,0:T(8,128)(2,1)} %bitcast.248, bf16[2,2,2048,512]{3,2,1,0:T(8,128)(2,1)} %bitcast.297), kind=kOutput, calls=%fused_computation.181 | convolution fusion | flops 8589934592 | bytes 25165824 | tf_op jit(solution)/shard_map/erd,epdf->eprf/dot_general | solution.py:62
  496.4 15.0 %fusion.17 = (bf16[2,2,1024,512]{3,2,1,0:T(8,128)(2,1)S(1)}, f32[2,1024,2,512]{3,1,2,0:T(8,128)}) fusion(f32[2,1024,2,512]{3,1,2,0:T(8,128)} %fusion.98, bf16[2,1024,2048,1]{2,1,3,0:T(8,128)(2,1)S(1)} %bitcast.251, bf16[2,2,2048,512]{3,2,1,0:T(8,128)(2,1)} %bitcast.299), kind=kOutput, calls=%fused_computation.31 | convolution fusion | flops 8602517504 | bytes 37748736 | tf_op jit(solution)/shard_map/erd,epdf->eprf/dot_general | solution.py:62
  511.4 19.9 %fusion.3 = (f32[2,1024]{1,0:T(2,128)S(1)}, f32[2,1024,2048,1]{2,1,3,0:T(8,128)}) fusion(f32[2,32,32,2048]{3,2,1,0:T(8,128)} %copy.247, bf16[2,2,1024,512]{3,2,1,0:T(8,128)(2,1)S(1)} %get-tuple-element.133, bf16[2,2,512,2048]{3,2,1,0:T(8,128)(2,1)} %bitcast.295), kind=kOutput, calls=%fused_computation.8 | convolution fusion | flops 8598321152 | bytes 46145536 | tf_op jit(solution)/shard_map/eprf,epfd->erd/dot_general | solution.py:62
  531.4 11.0 fusion.97
  545.6 17.0 %fusion.2 = (bf16[2,1024,2048]{2,1,0:T(8,128)(2,1)}, bf16[2,1024,2048]{2,1,0:T(8,128)(2,1)}) fusion(f32[2,32,32,2048]{3,2,1,0:T(8,128)} %copy.247, f32[2,1024]{1,0:T(2,128)S(1)} %mul.567, f32[2,1024,2048,1]{2,1,3,0:T(8,128)} %get-tuple-element.136), kind=kLoop, calls=%fused_computation.7 | loop fusion | flops 16777216 | bytes 50339840 | tf_op jit(solution)/shard_map/convert_element_type | solution.py:166
  562.6 18.9 %fusion.16 = (bf16[2,2,1024,512]{3,2,1,0:T(8,128)(2,1)}, bf16[2,2,1024,512]{3,2,1,0:T(8,128)(2,1)S(1)}) fusion(f32[2,1024,2,512]{3,1,2,0:T(8,128)} %fusion.98, f32[2,1024,2,512]{3,1,2,0:T(8,128)} %get-tuple-element.134, bf16[2,2,512,2048]{3,2,1,0:T(8,128)(2,1)} %bitcast.296, bf16[2,1024,2048]{2,1,0:T(8,128)(2,1)} %get-tuple-element.122), kind=kOutput, calls=%fused_computation.29 | convolution fusion | flops 8617197568 | bytes 41943040 | tf_op jit(solution)/shard_map/erd,epfd->eprf/dot_general | solution.py:62
  581.5 16.2 %fusion.99 = f32[2,1024,2048,1]{2,1,3,0:T(8,128)} fusion(bf16[2,2,1024,512]{3,2,1,0:T(8,128)(2,1)S(1)} %get-tuple-element.98, bf16[2,2,2048,512]{3,2,1,0:T(8,128)(2,1)} %bitcast.298), kind=kOutput, calls=%fused_computation.182 | convolution fusion | flops 8589934592 | bytes 29360128 | tf_op jit(solution)/shard_map/eprf,epdf->erd/dot_general | solution.py:62
  597.6 16.9 %fusion.1 = bf16[2,1024,2048]{2,1,0:T(8,128)(2,1)} fusion(f32[2,1024,2048,1]{2,1,3,0:T(8,128)} %fusion.99, bf16[2,2,1024,512]{3,2,1,0:T(8,128)(2,1)} %get-tuple-element.97, bf16[2,2,2048,512]{3,2,1,0:T(8,128)(2,1)} %bitcast.300), kind=kOutput, calls=%fused_computation.4 | convolution fusion | flops 8598323200 | bytes 37748736 | tf_op jit(solution)/shard_map/eprf,epdf->erd/dot_general | solution.py:62
  614.6 10.7 bitcast_convert_fusion
  630.7 11.0 all-to-all-done.2
  641.9 167.0 %reduce-scatter.8.cloned.1.call-done = bf16[128,2048]{1,0:T(8,128)(2,1)} async-done(((bf16[4096,2048]{1,0:T(8,128)(2,1)}), bf16[128,2048]{1,0:T(8,128)(2,1)}) %reduce-scatter.8.cloned.1.call-update) | async-done | bytes 524304 | tf_op jit(solution)/shard_map/reduce_scatter | solution.py:186
  812.1 74.1 %all-gather.15.cloned.1.call-done = bf16[1024,2048]{1,0:T(8,128)(2,1)} async-done(((bf16[128,2048]{1,0:T(8,128)(2,1)}), bf16[1024,2048]{1,0:T(8,128)(2,1)}) %all-gather.15.cloned.1.call-update) | async-done | bytes 4194320 | tf_op jit(solution)/shard_map/all_gather | solution.py:211
  886.2 4.1 multiply_reduce_fusion.1
  890.3 5.9 fusion.39
  906.2 6.8 fusion.47
  913.0 3.4 copy.262
  916.4 8.0 convolution_convert_fusion
  924.5 11.1 bitcast_convert_fusion.1
  937.0 16.9 %fusion.101 = f32[2,2,512,2048]{3,2,1,0:T(8,128)} fusion(bf16[2,2,1024,512]{3,2,1,0:T(8,128)(2,1)} %copy-done.34, bf16[2,1024,2048,1]{2,1,3,0:T(8,128)(2,1)} %bitcast.249), kind=kOutput, calls=%fused_computation.184 | convolution fusion | flops 8589934592 | bytes 29360128 | tf_op jit(solution)/shard_map/erd,eprf->epdf/dot_general | solution.py:62
  956.6 16.5 %fusion.102 = f32[2,2,512,2048]{3,2,1,0:T(8,128)} fusion(bf16[2,2,1024,512]{3,2,1,0:T(8,128)(2,1)} %get-tuple-element.97, bf16[2,1024,2048,1]{2,1,3,0:T(8,128)(2,1)} %bitcast.250), kind=kOutput, calls=%fused_computation.185 | convolution fusion | flops 8589934592 | bytes 29360128 | tf_op jit(solution)/shard_map/erd,eprf->epdf/dot_general | solution.py:62
  973.9 5.7 all-to-all-start.3
  979.7 16.6 %fusion.9 = f32[2,2,512,2048]{3,2,1,0:T(8,128)} fusion(bf16[2,2,1024,512]{3,2,1,0:T(8,128)(2,1)} %copy-done.33, bf16[2,1024,2048]{2,1,0:T(8,128)(2,1)} %get-tuple-element.122), kind=kOutput, calls=%fused_computation.20 | convolution fusion | flops 8589934592 | bytes 29360128 | tf_op jit(solution)/shard_map/eprf,erd->epfd/dot_general | solution.py:62
  996.3 16.4 %copy.269 = f32[4,2048,512]{2,1,0:T(8,128)} copy(f32[4,2048,512]{1,2,0:T(8,128)} %bitcast.240) | data formatting | bytes 33554432
  1012.6 16.5 %copy.270 = f32[4,2048,512]{2,1,0:T(8,128)} copy(f32[4,2048,512]{1,2,0:T(8,128)} %bitcast.241) | data formatting | bytes 33554432
  1029.1 42.9 %all_gather.35 = bf16[4096,64]{0,1:T(8,128)(2,1)S(1)} all-gather(bf16[128,64]{0,1:T(8,128)(2,1)S(1)} %multiply_convert_fusion.2), channel_id=1, replica_groups=mesh['seq'=8,'fsdp'=4] {'seq','fsdp'}, dimensions={0}, use_global_device_ids=true | all-gather | bytes 540672 | tf_op jit(solution)/shard_map/all_gather | solution.py:204
  1074.6 21.2 %reduce-scatter.10.cloned.1.call-done = bf16[128,2048]{1,0:T(8,128)(2,1)} async-done(((bf16[1024,2048]{1,0:T(8,128)(2,1)}), bf16[128,2048]{1,0:T(8,128)(2,1)}) %reduce-scatter.10.cloned.1.call-update) | async-done | bytes 524304 | tf_op jit(solution)/shard_map/reduce_scatter | solution.py:225
  1097.6 45.8 %all-reduce = f32[2,32,64]{2,0,1:T(2,128)S(1)} all-reduce(f32[2,32,64]{2,0,1:T(2,128)S(1)} %pad_maximum_fusion.7), channel_id=9, replica_groups=mesh['seq'=8,'fsdp'=4] {'seq','fsdp'}, use_global_device_ids=true, to_apply=%region_27.28.clone | all-reduce | flops 4096 | bytes 32768
  1144.0 138.5 %reduce-scatter.6.cloned.1.call-done = bf16[128,2048]{1,0:T(8,128)(2,1)} async-done(((bf16[4096,2048]{1,0:T(8,128)(2,1)}), bf16[128,2048]{1,0:T(8,128)(2,1)}) %reduce-scatter.6.cloned.1.call-update) | async-done | bytes 524304 | tf_op jit(solution)/shard_map/reduce_scatter | solution.py:195
  1293.2 25.0 %reduce-scatter.14.cloned.1.call-done = f32[64,2048]{1,0:T(8,128)} async-done(((f32[256,2048]{1,0:T(8,128)}), f32[64,2048]{1,0:T(8,128)}) %reduce-scatter.14.cloned.1.call-update) | async-done | bytes 524304 | tf_op jit(solution)/shard_map/reduce_scatter | solution.py:213
  (184 shorter events, 71.4 us)
Async XLA Ops:
  7.2 67.9 %all-gather.19.cloned.1.call-start = ((), (), s32[]{:S(2)}) async-start(), calls=%async_computation.18 | async-start | bytes 4587520 | tf_op jit(solution)/shard_map/all_gather | solution.py:121
  44.7 105.3 %all-gather.17.cloned.1.call-start = ((), (), s32[]{:S(2)}) async-start(), calls=%async_computation.17 | async-start | bytes 4718592 | tf_op jit(solution)/shard_map/all_gather | solution.py:101
  45.5 185.9 %all-gather.11.cloned.1.call-start = ((), (), s32[]{:S(2)}) async-start(), calls=%async_computation.9 | async-start | bytes 8650752 | tf_op jit(solution)/shard_map/all_gather | solution.py:126
  46.2 301.5 %all-gather.21.cloned.1.call-start = ((), (), s32[]{:S(2)}) async-start(), calls=%async_computation.19 | async-start | bytes 17301504 | tf_op jit(solution)/shard_map/all_gather | solution.py:128
  46.8 416.2 %all-gather.13.cloned.1.call-start = ((), (), s32[]{:S(2)}) async-start(), calls=%async_computation.10 | async-start | bytes 17301504 | tf_op jit(solution)/shard_map/all_gather | solution.py:147
  49.9 121.3 %copy-start.6 = (f32[1024,64]{1,0:T(8,128)}, f32[1024,64]{1,0:T(8,128)S(1)}, u32[]{:S(2)}) copy-start(f32[1024,64]{1,0:T(8,128)S(1)} %get-tuple-element.126) | copy-start | bytes 786436
  77.7 1.8 copy-start.4
  80.2 72.9 %copy-start.22 = (f32[2048]{0:T(1024)}, f32[2048]{0:T(1024)S(1)}, u32[]{:S(2)}) copy-start(f32[2048]{0:T(1024)S(1)} %get-tuple-element.85) | copy-start | bytes 24580
  80.2 156.0 %copy-start.20 = (f32[2048]{0:T(1024)}, f32[2048]{0:T(1024)S(1)}, u32[]{:S(2)}) copy-start(f32[2048]{0:T(1024)S(1)} %get-tuple-element.84) | copy-start | bytes 24580
  160.4 23.6 %copy-start.10 = (bf16[1024,256]{0,1:T(8,128)(2,1)}, bf16[1024,256]{0,1:T(8,128)(2,1)S(1)}, u32[]{:S(2)}) copy-start(bf16[1024,256]{0,1:T(8,128)(2,1)S(1)} %slice.127) | copy-start | bytes 1572868
  184.0 47.4 %copy-start.2 = (bf16[1,128,2048]{2,1,0:T(8,128)(2,1)S(1)}, bf16[1,128,2048]{2,1,0:T(8,128)(2,1)}, u32[]{:S(2)}) copy-start(bf16[1,128,2048]{2,1,0:T(8,128)(2,1)} %param.13) | copy-start | bytes 1572868
  231.4 6.8 copy-start.24
  236.2 1.0 copy-start
  236.2 42.8 %copy-start.30 = (f32[128]{0:T(128)}, f32[128]{0:T(128)S(1)}, u32[]{:S(2)}) copy-start(f32[128]{0:T(128)S(1)} %get-tuple-element.129) | copy-start | bytes 1540
  236.2 42.8 %copy-start.26 = (f32[128]{0:T(128)}, f32[128]{0:T(128)S(1)}, u32[]{:S(2)}) copy-start(f32[128]{0:T(128)S(1)} %fusion.86) | copy-start | bytes 1540
  238.1 570.7 %reduce-scatter.8.cloned.1.call-start = ((), (), s32[]{:S(2)}) async-start(), calls=%async_computation.12 | async-start | bytes 17301504 | tf_op jit(solution)/shard_map/reduce_scatter | solution.py:186
  480.7 15.8 %copy-start.5 = (bf16[2,32,32,2048]{3,2,1,0:T(8,128)(2,1)S(1)}, bf16[2,32,32,2048]{3,2,1,0:T(8,128)(2,1)}, u32[]{:S(2)}) copy-start(bf16[2,32,32,2048]{3,2,1,0:T(8,128)(2,1)} %copy.245) | copy-start | bytes 25165828
  511.4 19.9 %copy-start.33 = (bf16[2,2,1024,512]{3,2,1,0:T(8,128)(2,1)}, bf16[2,2,1024,512]{3,2,1,0:T(8,128)(2,1)S(1)}, u32[]{:S(2)}) copy-start(bf16[2,2,1024,512]{3,2,1,0:T(8,128)(2,1)S(1)} %get-tuple-element.133) | copy-start | bytes 12582916
  581.5 16.2 %copy-start.34 = (bf16[2,2,1024,512]{3,2,1,0:T(8,128)(2,1)}, bf16[2,2,1024,512]{3,2,1,0:T(8,128)(2,1)S(1)}, u32[]{:S(2)}) copy-start(bf16[2,2,1024,512]{3,2,1,0:T(8,128)(2,1)S(1)} %get-tuple-element.98) | copy-start | bytes 12582916
  625.3 1.0 copy-start.8
  625.3 16.3 %copy-start.25 = (s32[1,128,8]{1,2,0:T(8,128)S(1)}, s32[1,128,8]{1,2,0:T(8,128)}, u32[]{:S(2)}) copy-start(s32[1,128,8]{1,2,0:T(8,128)} %param.15) | copy-start | bytes 12292
  625.3 183.5 %copy-start.1 = (f32[128,2048]{1,0:T(8,128)S(1)}, f32[128,2048]{1,0:T(8,128)}, u32[]{:S(2)}) copy-start(f32[128,2048]{1,0:T(8,128)} %copy-done) | copy-start | bytes 3145732
  625.3 183.5 %copy-start.21 = (f32[2048]{0:T(1024)S(1)}, f32[2048]{0:T(1024)}, u32[]{:S(2)}) copy-start(f32[2048]{0:T(1024)} %copy-done.20) | copy-start | bytes 24580
  625.3 183.5 %copy-start.27 = (f32[128]{0:T(128)S(1)}, f32[128]{0:T(128)}, u32[]{:S(2)}) copy-start(f32[128]{0:T(128)} %copy-done.26) | copy-start | bytes 1540
  625.3 185.3 %copy-start.31 = (f32[128]{0:T(128)S(1)}, f32[128]{0:T(128)}, u32[]{:S(2)}) copy-start(f32[128]{0:T(128)} %copy-done.30) | copy-start | bytes 1540
  625.4 185.3 %copy-start.9 = (bf16[1,128,2048]{2,1,0:T(8,128)(2,1)S(1)}, bf16[1,128,2048]{2,1,0:T(8,128)(2,1)}, u32[]{:S(2)}) copy-start(bf16[1,128,2048]{2,1,0:T(8,128)(2,1)} %param.14) | copy-start | bytes 1572868
  627.8 13.9 %all-to-all-start.2 = ((f32[32,2,128]{2,1,0:T(2,128)}), f32[32,2,128]{2,1,0:T(2,128)S(1)}, u32[]{:S(2)}, u32[]{:S(2)}) async-start(f32[32,2,128]{2,1,0:T(2,128)} %get-tuple-element.92), calls=%async_computation.4 | async-start | bytes 65536 | tf_op jit(solution)/shard_map/all_to_all | solution.py:191
  630.6 255.6 %all-gather.15.cloned.1.call-start = ((), (), s32[]{:S(2)}) async-start(), calls=%async_computation.13 | async-start | bytes 4718592 | tf_op jit(solution)/shard_map/all_gather | solution.py:211
  811.9 162.1 %reduce-scatter.12.cloned.1.call-start = ((), (), s32[]{:S(2)}) async-start(), calls=%async_computation.15 | async-start | bytes 7864320 | tf_op jit(solution)/shard_map/reduce_scatter | solution.py:230
  812.1 84.1 %copy-start.11 = (bf16[1024,256]{0,1:T(8,128)(2,1)S(1)}, bf16[1024,256]{0,1:T(8,128)(2,1)}, u32[]{:S(2)}) copy-start(bf16[1024,256]{0,1:T(8,128)(2,1)} %copy-done.10) | copy-start | bytes 1572868
  886.2 9.9 slice-start
  890.3 5.9 slice-start.1
  896.2 1.4 copy-start.14
  896.2 1.4 copy-start.15
  896.2 3.4 copy-start.12
  896.2 3.4 copy-start.13
  897.6 3.4 copy-start.7
  897.6 3.4 copy-start.16
  899.7 6.6 copy-start.23
  899.7 6.5 copy-start.29
  913.0 3.5 copy-start.19
  916.4 179.5 %reduce-scatter.10.cloned.1.call-start = ((), (), s32[]{:S(2)}) async-start(), calls=%async_computation.14 | async-start | bytes 4718592 | tf_op jit(solution)/shard_map/reduce_scatter | solution.py:225
  924.5 358.0 %reduce-scatter.6.cloned.1.call-start = ((), (), s32[]{:S(2)}) async-start(), calls=%async_computation.11 | async-start | bytes 17301504 | tf_op jit(solution)/shard_map/reduce_scatter | solution.py:195
  935.6 1.2 copy-start.3
  935.6 382.6 %reduce-scatter.14.cloned.1.call-start = ((), (), s32[]{:S(2)}) async-start(), calls=%async_computation.16 | async-start | bytes 2621440 | tf_op jit(solution)/shard_map/reduce_scatter | solution.py:213
  937.0 17.0 %copy-start.18 = (bf16[2,128,1024]{2,1,0:T(8,128)(2,1)S(1)}, bf16[2,128,1024]{2,1,0:T(8,128)(2,1)}, u32[]{:S(2)}) copy-start(bf16[2,128,1024]{2,1,0:T(8,128)(2,1)} %copy-done.17) | copy-start | bytes 1572868
  937.0 17.0 %copy-start.32 = (bf16[1024,2048]{1,0:T(8,128)(2,1)S(1)}, bf16[1024,2048]{1,0:T(8,128)(2,1)}, u32[]{:S(2)}) copy-start(bf16[1024,2048]{1,0:T(8,128)(2,1)} %all-gather.15.cloned.1.call-done) | copy-start | bytes 12582916
  973.9 311.4 %all-to-all-start.3 = ((f32[8,64,768]{2,1,0:T(8,128)}), f32[8,64,768]{2,1,0:T(8,128)}, u32[]{:S(2)}, u32[]{:S(2)}) async-start(f32[8,64,768]{2,1,0:T(8,128)} %bitcast.270), calls=%async_computation.7 | async-start | bytes 3145728 | tf_op jit(solution)/shard_map/all_to_all | solution.py:231
  (2 other events, 1.4 us)
Sparse Core Ops, SparseCore 0:
  44.9 30.1 all-gather.18
  77.2 72.7 all-gather.16
  152.9 78.4 all-gather.10
  234.1 113.5 all-gather.20
  350.5 112.5 all-gather.12
  625.5 183.2 reduce-scatter.7
  812.0 74.2 all-gather.14
  916.5 57.3 reduce-scatter.11
  977.6 118.2 reduce-scatter.9
  1098.0 184.4 reduce-scatter.5
  1285.6 32.5 reduce-scatter.13
where the time goes:
time: 1340 us; the launch traced here: 1320 us
  waiting for transfers between devices  719 us (54%)
  matrix products  265 us (20%)
  blocking collectives  188 us (14%)
  local copies, waits for them, and re-layouts  88.1 us (7%)
  other arithmetic  40.5 us (3%)
  between operations  14.8 us (1%)
    dot_general x19, matrix products, ein(): return jnp.einsum(spec, *args, preferred_element_type=f32)  206 us
    reduce_scatter x1, waiting for transfers between devices, body(): lax.psum_scatter(spread(back), AXES, scatter_dimension=0, tiled=True)  167 us
    reduce_scatter x1, waiting for transfers between devices, body(): lax.psum_scatter(spread(w_rows * out), AXES, scatter_dimension=0, tiled=T...  139 us
    all_gather x1, waiting for transfers between devices, body(): x_all = lax.all_gather(normed_mid, AXES, axis=0, tiled=True)  102 us
    all_gather x1, waiting for transfers between devices, body(): lax.all_gather(resid_grad.astype(bf16), 'seq', axis=0, tiled=True)  74.1 us
    all_gather x1, waiting for transfers between devices, body(): x_seq = lax.all_gather(x_own, 'seq', axis=0, tiled=True)  69.8 us
    all_gather x1, waiting for transfers between devices, body(): cot_all = lax.all_gather(cot_own, AXES, axis=0, tiled=True)  68.4 us
    unnamed x88, local copies, waits for them, and re-layouts  51 us
  transfers between devices with their start and end apart: 13, of which 12 were waited for; matrix products, arithmetic and copies ran while one was open for 14% of the time, Pallas kernels for 0%

commit v1 on v0

--- a/solution.py
+++ b/solution.py
@@ -98,7 +98,24 @@
     cot_own = cotangent[0]
     chosen = routes[0]
     routes_all = lax.all_gather(chosen, AXES, axis=0, tiled=True)
-    x_seq = lax.all_gather(x_own, "seq", axis=0, tiled=True)
+    count, here, width_2 = (lax.axis_size("seq"), lax.axis_index("seq"), x_own.shape[0])
+    right_2 = [(i, (i + 1) % count) for i in range(count)]
+    left_2 = [(i, (i - 1) % count) for i in range(count)]
+    out_2 = jnp.zeros((*x_own.shape[:0], count * width_2, *x_own.shape[0 + 1 :]), x_own.dtype)
+    out_2 = lax.dynamic_update_slice_in_dim(out_2, x_own, here * width_2, axis=0)
+    from_left = from_right = x_own
+    halfway = count // 2
+    for lap in range(1, halfway + 1):
+        from_left = lax.ppermute(from_left, "seq", right_2)
+        out_2 = lax.dynamic_update_slice_in_dim(
+            out_2, from_left, (here - lap) % count * width_2, axis=0
+        )
+        if lap < count - halfway:
+            from_right = lax.ppermute(from_right, "seq", left_2)
+            out_2 = lax.dynamic_update_slice_in_dim(
+                out_2, from_right, (here + lap) % count * width_2, axis=0
+            )
+    x_seq = out_2
     small = jnp.concatenate(
         [
             router_weight,

time: 1340 us -> 1280 us (0.955)
  waiting for transfers between devices: 719 us -> 650 us
  starting transfers between devices: 9.6 us -> 26.3 us
    all_gather x1 -> x0, waiting for transfers between devices: 69.8 us -> none  [body(): x_seq = lax.all_gather(x_own, 'seq', axis=0, tiled=True)]
    ppermute x0 -> x7, waiting for transfers between devices: none -> 67.9 us  [the longest x4 61.1 us: body(): from_left = lax.ppermute(from_left, 'seq', right_2)]
    all_gather x1, waiting for transfers between devices: 68.4 us -> 42.4 us  [body(): cot_all = lax.all_gather(cot_own, AXES, axis=0, tiled=True)]
    all_gather x1, waiting for transfers between devices: 25.2 us -> 0.02 us  [body(): lax.all_gather(moved, 'fsdp', axis=1).reshape(width, 3 * cols + 128)]
    ppermute x0 -> x7, starting transfers between devices: none -> 16.9 us  [the longest x4 8.74 us: body(): from_left = lax.ppermute(from_left, 'seq', right_2)]
    all_gather x1, waiting for transfers between devices: 14.1 us -> 0.01 us  [body(): out_full = lax.all_gather(output_weight, AXES, axis=0, tiled=True)]
    unnamed x88 -> x90, local copies, waits for them, and re-layouts: 51 us -> 49.9 us
  transfers between devices with their start and end apart: 13 -> 19, of which waited for: 12 -> 14; matrix products, arithmetic and copies ran while one was open for 14% -> 15% of each run, Pallas kernels for 0% -> 0%
where the time goes in v1:
time: 1280 us
  waiting for transfers between devices  650 us (51%)
  matrix products  264 us (21%)
  blocking collectives  183 us (14%)
  local copies, waits for them, and re-layouts  96.1 us (8%)
  other arithmetic  40.6 us (3%)
  starting transfers between devices  26.3 us (2%)
  between operations  15.1 us (1%)
    dot_general x19, matrix products, ein(): return jnp.einsum(spec, *args, preferred_element_type=f32)  205 us
    reduce_scatter x1, waiting for transfers between devices, body(): lax.psum_scatter(spread(back), AXES, scatter_dimension=0, tiled=True)  166 us
    reduce_scatter x1, waiting for transfers between devices, body(): lax.psum_scatter(spread(w_rows * out), AXES, scatter_dimension=0, tiled=T...  139 us
    all_gather x1, waiting for transfers between devices, body(): x_all = lax.all_gather(normed_mid, AXES, axis=0, tiled=True)  102 us
    all_gather x1, waiting for transfers between devices, body(): lax.all_gather(resid_grad.astype(bf16), 'seq', axis=0, tiled=True)  74.1 us
    ppermute x4, waiting for transfers between devices, body(): from_left = lax.ppermute(from_left, 'seq', right_2)  61.1 us
    unnamed x90, local copies, waits for them, and re-layouts  49.9 us
    unnamed x1, blocking collectives  45.3 us
  transfers between devices with their start and end apart: 19, of which 14 were waited for; matrix products, arithmetic and copies ran while one was open for 15% of the time, Pallas kernels for 0%

profile of v1, /device:TPU:0, one launch (start us, length us, event | category | flops | bytes accessed | tf_op | source)
XLA Modules:
  0.0 1275.6 jit_solution(10258727008049498208)
XLA Ops:
  13.0 30.4 %all_to_all.34 = bf16[8,64,896]{2,1,0:T(8,128)(2,1)S(1)} all-to-all(bf16[8,64,896]{2,1,0:T(8,128)(2,1)S(1)} %copy.233), channel_id=1, replica_groups=mesh['seq'=8,'fsdp'=4] {'seq'}, dimensions={0} | all-to-all | bytes 1835008 | tf_op jit(solution)/shard_map/all_to_all | solution.py:137
  47.5 3.6 collective-permute-start.1
  51.1 18.0 %collective-permute-done = bf16[128,2048]{1,0:T(8,128)(2,1)S(1)} collective-permute-done((bf16[128,2048]{1,0:T(8,128)(2,1)S(1)}, bf16[128,2048]{1,0:T(8,128)(2,1)S(1)}, u32[]{:S(2)}, u32[]{:S(2)}) %collective-permute-start) | collective-permute-done | bytes 524320 | tf_op jit(solution)/shard_map/ppermute | solution.py:109
  80.3 14.1 %collective-permute-done.2 = bf16[128,2048]{1,0:T(8,128)(2,1)S(1)} collective-permute-done((bf16[128,2048]{1,0:T(8,128)(2,1)S(1)}, bf16[128,2048]{1,0:T(8,128)(2,1)S(1)}, u32[]{:S(2)}, u32[]{:S(2)}) %collective-permute-start.2) | collective-permute-done | bytes 524320 | tf_op jit(solution)/shard_map/ppermute | solution.py:109
  101.7 16.4 %collective-permute-done.4 = bf16[128,2048]{1,0:T(8,128)(2,1)S(1)} collective-permute-done((bf16[128,2048]{1,0:T(8,128)(2,1)S(1)}, bf16[128,2048]{1,0:T(8,128)(2,1)S(1)}, u32[]{:S(2)}, u32[]{:S(2)}) %collective-permute-start.4) | collective-permute-done | bytes 524320 | tf_op jit(solution)/shard_map/ppermute | solution.py:109
  122.4 6.7 collective-permute-done.5
  130.0 12.6 collective-permute-done.6
  151.0 5.8 fusion.30
  167.4 3.6 subtract_convert_fusion.3
  171.0 9.3 fusion.8
  180.3 4.1 fusion.36
  185.2 24.9 %all_to_all.35 = bf16[8,128,256]{1,2,0:T(8,128)(2,1)S(1)} all-to-all(bf16[8,128,256]{1,2,0:T(8,128)(2,1)S(1)} %copy.241), channel_id=1, replica_groups=mesh['seq'=8,'fsdp'=4] {'seq'}, dimensions={0} | all-to-all | bytes 1048576 | tf_op jit(solution)/shard_map/all_to_all | solution.py:160
  210.1 4.8 multiply_reduce_fusion.3
  216.9 40.1 %all-gather.1 = s32[1,4096,8]{1,2,0:T(8,128)S(1)} all-gather(s32[1,128,8]{1,2,0:T(8,128)S(1)} %copy-done.25), channel_id=3, replica_groups=mesh['seq'=8,'fsdp'=4] {'seq','fsdp'}, dimensions={1}, use_global_device_ids=true | all-gather | bytes 135168 | tf_op jit(solution)/shard_map/all_gather | solution.py:100
  257.4 42.4 %all-gather.17.cloned.1.call-done = bf16[1,4096,2048]{2,1,0:T(8,128)(2,1)} async-done(((bf16[1,128,2048]{2,1,0:T(8,128)(2,1)}), bf16[1,4096,2048]{2,1,0:T(8,128)(2,1)}) %all-gather.17.cloned.1.call-update) | async-done | bytes 16777232 | tf_op jit(solution)/shard_map/all_gather | solution.py:145
  299.8 7.0 convolution_bitcast_fusion
  306.8 6.2 copy.247
  313.1 102.0 %all-gather.11.cloned.1.call-done = bf16[4096,2048]{1,0:T(8,128)(2,1)} async-done(((bf16[128,2048]{1,0:T(8,128)(2,1)}), bf16[4096,2048]{1,0:T(8,128)(2,1)}) %all-gather.11.cloned.1.call-update) | async-done | bytes 16777232 | tf_op jit(solution)/shard_map/all_gather | solution.py:164
  415.1 9.4 convert_bitcast_fusion
  424.5 8.3 copy.245
  432.7 15.8 %fusion.98 = f32[2,1024,2,512]{3,1,2,0:T(8,128)} fusion(bf16[2,1024,2048,1]{2,1,3,0:T(8,128)(2,1)} %bitcast.244, bf16[2,2,2048,512]{3,2,1,0:T(8,128)(2,1)} %bitcast.293), kind=kOutput, calls=%fused_computation.189 | convolution fusion | flops 8589934592 | bytes 25165824 | tf_op jit(solution)/shard_map/erd,epdf->eprf/dot_general | solution.py:62
  448.5 15.0 %fusion.17 = (bf16[2,2,1024,512]{3,2,1,0:T(8,128)(2,1)S(1)}, f32[2,1024,2,512]{3,1,2,0:T(8,128)}) fusion(f32[2,1024,2,512]{3,1,2,0:T(8,128)} %fusion.98, bf16[2,1024,2048,1]{2,1,3,0:T(8,128)(2,1)S(1)} %bitcast.247, bf16[2,2,2048,512]{3,2,1,0:T(8,128)(2,1)} %bitcast.295), kind=kOutput, calls=%fused_computation.31 | convolution fusion | flops 8602517504 | bytes 37748736 | tf_op jit(solution)/shard_map/erd,epdf->eprf/dot_general | solution.py:62
  463.5 19.9 %fusion.3 = (f32[2,1024]{1,0:T(2,128)S(1)}, f32[2,1024,2048,1]{2,1,3,0:T(8,128)}) fusion(f32[2,32,32,2048]{3,2,1,0:T(8,128)} %copy.247, bf16[2,2,1024,512]{3,2,1,0:T(8,128)(2,1)S(1)} %get-tuple-element.133, bf16[2,2,512,2048]{3,2,1,0:T(8,128)(2,1)} %bitcast.291), kind=kOutput, calls=%fused_computation.8 | convolution fusion | flops 8598321152 | bytes 46145536 | tf_op jit(solution)/shard_map/eprf,epfd->erd/dot_general | solution.py:62
  483.5 11.0 fusion.97
  497.7 17.0 %fusion.2 = (bf16[2,1024,2048]{2,1,0:T(8,128)(2,1)}, bf16[2,1024,2048]{2,1,0:T(8,128)(2,1)}) fusion(f32[2,32,32,2048]{3,2,1,0:T(8,128)} %copy.247, f32[2,1024]{1,0:T(2,128)S(1)} %mul.599, f32[2,1024,2048,1]{2,1,3,0:T(8,128)} %get-tuple-element.136), kind=kLoop, calls=%fused_computation.7 | loop fusion | flops 16777216 | bytes 50339840 | tf_op jit(solution)/shard_map/convert_element_type | solution.py:183
  514.6 18.7 %fusion.16 = (bf16[2,2,1024,512]{3,2,1,0:T(8,128)(2,1)}, bf16[2,2,1024,512]{3,2,1,0:T(8,128)(2,1)S(1)}) fusion(f32[2,1024,2,512]{3,1,2,0:T(8,128)} %fusion.98, f32[2,1024,2,512]{3,1,2,0:T(8,128)} %get-tuple-element.134, bf16[2,2,512,2048]{3,2,1,0:T(8,128)(2,1)} %bitcast.292, bf16[2,1024,2048]{2,1,0:T(8,128)(2,1)} %get-tuple-element.122), kind=kOutput, calls=%fused_computation.29 | convolution fusion | flops 8617197568 | bytes 41943040 | tf_op jit(solution)/shard_map/erd,epfd->eprf/dot_general | solution.py:62
  533.3 16.2 %fusion.99 = f32[2,1024,2048,1]{2,1,3,0:T(8,128)} fusion(bf16[2,2,1024,512]{3,2,1,0:T(8,128)(2,1)S(1)} %get-tuple-element.98, bf16[2,2,2048,512]{3,2,1,0:T(8,128)(2,1)} %bitcast.294), kind=kOutput, calls=%fused_computation.190 | convolution fusion | flops 8589934592 | bytes 29360128 | tf_op jit(solution)/shard_map/eprf,epdf->erd/dot_general | solution.py:62
  549.5 16.9 %fusion.1 = bf16[2,1024,2048]{2,1,0:T(8,128)(2,1)} fusion(f32[2,1024,2048,1]{2,1,3,0:T(8,128)} %fusion.99, bf16[2,2,1024,512]{3,2,1,0:T(8,128)(2,1)} %get-tuple-element.97, bf16[2,2,2048,512]{3,2,1,0:T(8,128)(2,1)} %bitcast.296), kind=kOutput, calls=%fused_computation.4 | convolution fusion | flops 8598323200 | bytes 37748736 | tf_op jit(solution)/shard_map/eprf,epdf->erd/dot_general | solution.py:62
  566.5 10.7 bitcast_convert_fusion
  582.5 11.0 all-to-all-done.2
  593.7 165.6 %reduce-scatter.8.cloned.1.call-done = bf16[128,2048]{1,0:T(8,128)(2,1)} async-done(((bf16[4096,2048]{1,0:T(8,128)(2,1)}), bf16[128,2048]{1,0:T(8,128)(2,1)}) %reduce-scatter.8.cloned.1.call-update) | async-done | bytes 524304 | tf_op jit(solution)/shard_map/reduce_scatter | solution.py:203
  762.7 74.1 %all-gather.13.cloned.1.call-done = bf16[1024,2048]{1,0:T(8,128)(2,1)} async-done(((bf16[128,2048]{1,0:T(8,128)(2,1)}), bf16[1024,2048]{1,0:T(8,128)(2,1)}) %all-gather.13.cloned.1.call-update) | async-done | bytes 4194320 | tf_op jit(solution)/shard_map/all_gather | solution.py:228
  836.7 4.1 multiply_reduce_fusion.1
  840.8 5.9 fusion.39
  856.7 6.9 fusion.47
  867.1 8.0 convolution_convert_fusion
  875.2 11.1 bitcast_convert_fusion.1
  887.7 16.9 %fusion.101 = f32[2,2,512,2048]{3,2,1,0:T(8,128)} fusion(bf16[2,2,1024,512]{3,2,1,0:T(8,128)(2,1)} %copy-done.35, bf16[2,1024,2048,1]{2,1,3,0:T(8,128)(2,1)} %bitcast.245), kind=kOutput, calls=%fused_computation.192 | convolution fusion | flops 8589934592 | bytes 29360128 | tf_op jit(solution)/shard_map/erd,eprf->epdf/dot_general | solution.py:62
  907.3 16.5 %fusion.102 = f32[2,2,512,2048]{3,2,1,0:T(8,128)} fusion(bf16[2,2,1024,512]{3,2,1,0:T(8,128)(2,1)} %get-tuple-element.97, bf16[2,1024,2048,1]{2,1,3,0:T(8,128)(2,1)} %bitcast.246), kind=kOutput, calls=%fused_computation.193 | convolution fusion | flops 8589934592 | bytes 29360128 | tf_op jit(solution)/shard_map/erd,eprf->epdf/dot_general | solution.py:62
  924.6 5.8 all-to-all-start.3
  930.4 16.6 %fusion.9 = f32[2,2,512,2048]{3,2,1,0:T(8,128)} fusion(bf16[2,2,1024,512]{3,2,1,0:T(8,128)(2,1)} %copy-done.34, bf16[2,1024,2048]{2,1,0:T(8,128)(2,1)} %get-tuple-element.122), kind=kOutput, calls=%fused_computation.20 | convolution fusion | flops 8589934592 | bytes 29360128 | tf_op jit(solution)/shard_map/eprf,erd->epfd/dot_general | solution.py:62
  947.0 16.4 %copy.269 = f32[4,2048,512]{2,1,0:T(8,128)} copy(f32[4,2048,512]{1,2,0:T(8,128)} %bitcast.234) | data formatting | bytes 33554432
  963.3 16.4 %copy.270 = f32[4,2048,512]{2,1,0:T(8,128)} copy(f32[4,2048,512]{1,2,0:T(8,128)} %bitcast.235) | data formatting | bytes 33554432
  979.8 42.8 %all_gather.31 = bf16[4096,64]{0,1:T(8,128)(2,1)S(1)} all-gather(bf16[128,64]{0,1:T(8,128)(2,1)S(1)} %multiply_convert_fusion.2), channel_id=1, replica_groups=mesh['seq'=8,'fsdp'=4] {'seq','fsdp'}, dimensions={0}, use_global_device_ids=true | all-gather | bytes 540672 | tf_op jit(solution)/shard_map/all_gather | solution.py:221
  1025.2 21.3 %reduce-scatter.10.cloned.1.call-done = bf16[128,2048]{1,0:T(8,128)(2,1)} async-done(((bf16[1024,2048]{1,0:T(8,128)(2,1)}), bf16[128,2048]{1,0:T(8,128)(2,1)}) %reduce-scatter.10.cloned.1.call-update) | async-done | bytes 524304 | tf_op jit(solution)/shard_map/reduce_scatter | solution.py:242
  1048.3 45.3 %all-reduce = f32[2,32,64]{2,0,1:T(2,128)S(1)} all-reduce(f32[2,32,64]{2,0,1:T(2,128)S(1)} %pad_maximum_fusion.7), channel_id=8, replica_groups=mesh['seq'=8,'fsdp'=4] {'seq','fsdp'}, use_global_device_ids=true, to_apply=%region_27.28.clone | all-reduce | flops 4096 | bytes 32768
  1094.1 138.9 %reduce-scatter.6.cloned.1.call-done = bf16[128,2048]{1,0:T(8,128)(2,1)} async-done(((bf16[4096,2048]{1,0:T(8,128)(2,1)}), bf16[128,2048]{1,0:T(8,128)(2,1)}) %reduce-scatter.6.cloned.1.call-update) | async-done | bytes 524304 | tf_op jit(solution)/shard_map/reduce_scatter | solution.py:212
  1243.8 24.8 %reduce-scatter.14.cloned.1.call-done = f32[64,2048]{1,0:T(8,128)} async-done(((f32[256,2048]{1,0:T(8,128)}), f32[64,2048]{1,0:T(8,128)}) %reduce-scatter.14.cloned.1.call-update) | async-done | bytes 524304 | tf_op jit(solution)/shard_map/reduce_scatter | solution.py:230
  (206 shorter events, 101.3 us)
Async XLA Ops:
  7.2 39.2 %copy-start.2 = (bf16[1,128,2048]{2,1,0:T(8,128)(2,1)S(1)}, bf16[1,128,2048]{2,1,0:T(8,128)(2,1)}, u32[]{:S(2)}) copy-start(bf16[1,128,2048]{2,1,0:T(8,128)(2,1)} %param.13) | copy-start | bytes 1572868
  7.2 139.3 %all-gather.15.cloned.1.call-start = ((), (), s32[]{:S(2)}) async-start(), calls=%async_computation.17 | async-start | bytes 4587520 | tf_op jit(solution)/shard_map/all_gather | solution.py:138
  44.8 165.3 %all-gather.9.cloned.1.call-start = ((), (), s32[]{:S(2)}) async-start(), calls=%async_computation.9 | async-start | bytes 8650752 | tf_op jit(solution)/shard_map/all_gather | solution.py:143
  45.6 254.2 %all-gather.17.cloned.1.call-start = ((), (), s32[]{:S(2)}) async-start(), calls=%async_computation.18 | async-start | bytes 17301504 | tf_op jit(solution)/shard_map/all_gather | solution.py:145
  46.3 368.8 %all-gather.11.cloned.1.call-start = ((), (), s32[]{:S(2)}) async-start(), calls=%async_computation.10 | async-start | bytes 17301504 | tf_op jit(solution)/shard_map/all_gather | solution.py:164
  46.4 22.8 %collective-permute-start = (bf16[128,2048]{1,0:T(8,128)(2,1)S(1)}, bf16[128,2048]{1,0:T(8,128)(2,1)S(1)}, u32[]{:S(2)}, u32[]{:S(2)}) collective-permute-start(bf16[128,2048]{1,0:T(8,128)(2,1)S(1)} %bitcast.236), channel_id=1, source_target_pairs={{0,4},{4,8},{8,12},{12,16},{16,20},{20,24},{24,28},{28,0},{1,5},{5... | collective-permute-start | bytes 1572872 | tf_op jit(solution)/shard_map/ppermute | solution.py:109
  47.5 27.5 %collective-permute-start.1 = (bf16[128,2048]{1,0:T(8,128)(2,1)S(1)}, bf16[128,2048]{1,0:T(8,128)(2,1)S(1)}, u32[]{:S(2)}, u32[]{:S(2)}) collective-permute-start(bf16[128,2048]{1,0:T(8,128)(2,1)S(1)} %bitcast.237), channel_id=1, source_target_pairs={{0,28},{4,0},{8,4},{12,8},{16,12},{20,16},{24,20},{28,24},{1,29},{... | collective-permute-start | bytes 1572872 | tf_op jit(solution)/shard_map/ppermute | solution.py:114
  69.1 25.3 %collective-permute-start.2 = (bf16[128,2048]{1,0:T(8,128)(2,1)S(1)}, bf16[128,2048]{1,0:T(8,128)(2,1)S(1)}, u32[]{:S(2)}, u32[]{:S(2)}) collective-permute-start(bf16[128,2048]{1,0:T(8,128)(2,1)S(1)} %collective-permute-done), channel_id=1, source_target_pairs={{0,4},{4,8},{8,12},{12,16},{16,20},{20,24},{24,28},{28,0},{1,5},{5... | collective-permute-start | bytes 1572872 | tf_op jit(solution)/shard_map/ppermute | solution.py:109
  75.0 23.7 %collective-permute-start.3 = (bf16[128,2048]{1,0:T(8,128)(2,1)S(1)}, bf16[128,2048]{1,0:T(8,128)(2,1)S(1)}, u32[]{:S(2)}, u32[]{:S(2)}) collective-permute-start(bf16[128,2048]{1,0:T(8,128)(2,1)S(1)} %collective-permute-done.1), channel_id=1, source_target_pairs={{0,28},{4,0},{8,4},{12,8},{16,12},{20,16},{24,20},{28,24},{1,29},{... | collective-permute-start | bytes 1572872 | tf_op jit(solution)/shard_map/ppermute | solution.py:114
  80.3 87.0 %copy-start.6 = (f32[1024,64]{1,0:T(8,128)}, f32[1024,64]{1,0:T(8,128)S(1)}, u32[]{:S(2)}) copy-start(f32[1024,64]{1,0:T(8,128)S(1)} %get-tuple-element.126) | copy-start | bytes 786436
  94.5 23.7 %collective-permute-start.4 = (bf16[128,2048]{1,0:T(8,128)(2,1)S(1)}, bf16[128,2048]{1,0:T(8,128)(2,1)S(1)}, u32[]{:S(2)}, u32[]{:S(2)}) collective-permute-start(bf16[128,2048]{1,0:T(8,128)(2,1)S(1)} %collective-permute-done.2), channel_id=1, source_target_pairs={{0,4},{4,8},{8,12},{12,16},{16,20},{20,24},{24,28},{28,0},{1,5},{5... | collective-permute-start | bytes 1572872 | tf_op jit(solution)/shard_map/ppermute | solution.py:109
  98.7 30.5 %collective-permute-start.5 = (bf16[128,2048]{1,0:T(8,128)(2,1)S(1)}, bf16[128,2048]{1,0:T(8,128)(2,1)S(1)}, u32[]{:S(2)}, u32[]{:S(2)}) collective-permute-start(bf16[128,2048]{1,0:T(8,128)(2,1)S(1)} %collective-permute-done.3), channel_id=1, source_target_pairs={{0,28},{4,0},{8,4},{12,8},{16,12},{20,16},{24,20},{28,24},{1,29},{... | collective-permute-start | bytes 1572872 | tf_op jit(solution)/shard_map/ppermute | solution.py:114
  118.1 24.4 %collective-permute-start.6 = (bf16[128,2048]{1,0:T(8,128)(2,1)S(1)}, bf16[128,2048]{1,0:T(8,128)(2,1)S(1)}, u32[]{:S(2)}, u32[]{:S(2)}) collective-permute-start(bf16[128,2048]{1,0:T(8,128)(2,1)S(1)} %collective-permute-done.4), channel_id=1, source_target_pairs={{0,4},{4,8},{8,12},{12,16},{16,20},{20,24},{24,28},{28,0},{1,5},{5... | collective-permute-start | bytes 1572872 | tf_op jit(solution)/shard_map/ppermute | solution.py:109
  146.5 3.4 copy-start.29
  149.2 7.6 copy-start.4
  149.9 65.1 %copy-start.21 = (f32[2048]{0:T(1024)}, f32[2048]{0:T(1024)S(1)}, u32[]{:S(2)}) copy-start(f32[2048]{0:T(1024)S(1)} %get-tuple-element.84) | copy-start | bytes 24580
  156.9 23.4 %copy-start.10 = (bf16[1024,256]{0,1:T(8,128)(2,1)}, bf16[1024,256]{0,1:T(8,128)(2,1)S(1)}, u32[]{:S(2)}) copy-start(bf16[1024,256]{0,1:T(8,128)(2,1)S(1)} %slice.127) | copy-start | bytes 1572868
  171.0 9.3 copy-start.12
  210.1 6.8 copy-start.25
  214.9 42.1 %copy-start.31 = (f32[128]{0:T(128)}, f32[128]{0:T(128)S(1)}, u32[]{:S(2)}) copy-start(f32[128]{0:T(128)S(1)} %get-tuple-element.129) | copy-start | bytes 1540
  214.9 42.1 %copy-start.27 = (f32[128]{0:T(128)}, f32[128]{0:T(128)S(1)}, u32[]{:S(2)}) copy-start(f32[128]{0:T(128)S(1)} %fusion.86) | copy-start | bytes 1540
  216.9 542.5 %reduce-scatter.8.cloned.1.call-start = ((), (), s32[]{:S(2)}) async-start(), calls=%async_computation.12 | async-start | bytes 17301504 | tf_op jit(solution)/shard_map/reduce_scatter | solution.py:203
  432.7 15.8 %copy-start.5 = (bf16[2,32,32,2048]{3,2,1,0:T(8,128)(2,1)S(1)}, bf16[2,32,32,2048]{3,2,1,0:T(8,128)(2,1)}, u32[]{:S(2)}) copy-start(bf16[2,32,32,2048]{3,2,1,0:T(8,128)(2,1)} %copy.245) | copy-start | bytes 25165828
  463.5 19.9 %copy-start.34 = (bf16[2,2,1024,512]{3,2,1,0:T(8,128)(2,1)}, bf16[2,2,1024,512]{3,2,1,0:T(8,128)(2,1)S(1)}, u32[]{:S(2)}) copy-start(bf16[2,2,1024,512]{3,2,1,0:T(8,128)(2,1)S(1)} %get-tuple-element.133) | copy-start | bytes 12582916
  533.3 16.2 %copy-start.35 = (bf16[2,2,1024,512]{3,2,1,0:T(8,128)(2,1)}, bf16[2,2,1024,512]{3,2,1,0:T(8,128)(2,1)S(1)}, u32[]{:S(2)}) copy-start(bf16[2,2,1024,512]{3,2,1,0:T(8,128)(2,1)S(1)} %get-tuple-element.98) | copy-start | bytes 12582916
  577.2 16.3 %copy-start.26 = (s32[1,128,8]{1,2,0:T(8,128)S(1)}, s32[1,128,8]{1,2,0:T(8,128)}, u32[]{:S(2)}) copy-start(s32[1,128,8]{1,2,0:T(8,128)} %param.15) | copy-start | bytes 12292
  577.2 182.2 %copy-start.1 = (f32[128,2048]{1,0:T(8,128)S(1)}, f32[128,2048]{1,0:T(8,128)}, u32[]{:S(2)}) copy-start(f32[128,2048]{1,0:T(8,128)} %copy-done) | copy-start | bytes 3145732
  577.2 182.2 %copy-start.22 = (f32[2048]{0:T(1024)S(1)}, f32[2048]{0:T(1024)}, u32[]{:S(2)}) copy-start(f32[2048]{0:T(1024)} %copy-done.21) | copy-start | bytes 24580
  577.2 182.2 %copy-start.28 = (f32[128]{0:T(128)S(1)}, f32[128]{0:T(128)}, u32[]{:S(2)}) copy-start(f32[128]{0:T(128)} %copy-done.27) | copy-start | bytes 1540
  577.2 184.0 %copy-start.32 = (f32[128]{0:T(128)S(1)}, f32[128]{0:T(128)}, u32[]{:S(2)}) copy-start(f32[128]{0:T(128)} %copy-done.31) | copy-start | bytes 1540
  577.2 184.0 %copy-start.9 = (bf16[1,128,2048]{2,1,0:T(8,128)(2,1)S(1)}, bf16[1,128,2048]{2,1,0:T(8,128)(2,1)}, u32[]{:S(2)}) copy-start(bf16[1,128,2048]{2,1,0:T(8,128)(2,1)} %param.14) | copy-start | bytes 1572868
  579.6 13.9 %all-to-all-start.2 = ((f32[32,2,128]{2,1,0:T(2,128)}), f32[32,2,128]{2,1,0:T(2,128)S(1)}, u32[]{:S(2)}, u32[]{:S(2)}) async-start(f32[32,2,128]{2,1,0:T(2,128)} %get-tuple-element.92), calls=%async_computation.4 | async-start | bytes 65536 | tf_op jit(solution)/shard_map/all_to_all | solution.py:208
  582.5 254.3 %all-gather.13.cloned.1.call-start = ((), (), s32[]{:S(2)}) async-start(), calls=%async_computation.13 | async-start | bytes 4718592 | tf_op jit(solution)/shard_map/all_gather | solution.py:228
  762.4 162.2 %reduce-scatter.12.cloned.1.call-start = ((), (), s32[]{:S(2)}) async-start(), calls=%async_computation.15 | async-start | bytes 7864320 | tf_op jit(solution)/shard_map/reduce_scatter | solution.py:247
  762.6 84.0 %copy-start.11 = (bf16[1024,256]{0,1:T(8,128)(2,1)S(1)}, bf16[1024,256]{0,1:T(8,128)(2,1)}, u32[]{:S(2)}) copy-start(bf16[1024,256]{0,1:T(8,128)(2,1)} %copy-done.10) | copy-start | bytes 1572868
  836.7 9.9 slice-start
  840.8 5.9 slice-start.1
  846.7 3.4 copy-start.13
  846.7 3.4 copy-start.14
  850.1 6.5 copy-start.24
  850.2 6.5 copy-start.30
  863.7 3.5 copy-start.20
  867.1 179.5 %reduce-scatter.10.cloned.1.call-start = ((), (), s32[]{:S(2)}) async-start(), calls=%async_computation.14 | async-start | bytes 4718592 | tf_op jit(solution)/shard_map/reduce_scatter | solution.py:242
  875.1 357.9 %reduce-scatter.6.cloned.1.call-start = ((), (), s32[]{:S(2)}) async-start(), calls=%async_computation.11 | async-start | bytes 17301504 | tf_op jit(solution)/shard_map/reduce_scatter | solution.py:212
  886.3 382.2 %reduce-scatter.14.cloned.1.call-start = ((), (), s32[]{:S(2)}) async-start(), calls=%async_computation.16 | async-start | bytes 2621440 | tf_op jit(solution)/shard_map/reduce_scatter | solution.py:230
  887.7 16.9 %copy-start.19 = (bf16[2,128,1024]{2,1,0:T(8,128)(2,1)S(1)}, bf16[2,128,1024]{2,1,0:T(8,128)(2,1)}, u32[]{:S(2)}) copy-start(bf16[2,128,1024]{2,1,0:T(8,128)(2,1)} %copy-done.18) | copy-start | bytes 1572868
  887.7 16.9 %copy-start.33 = (bf16[1024,2048]{1,0:T(8,128)(2,1)S(1)}, bf16[1024,2048]{1,0:T(8,128)(2,1)}, u32[]{:S(2)}) copy-start(bf16[1024,2048]{1,0:T(8,128)(2,1)} %all-gather.13.cloned.1.call-done) | copy-start | bytes 12582916
  924.6 311.3 %all-to-all-start.3 = ((f32[8,64,768]{2,1,0:T(8,128)}), f32[8,64,768]{2,1,0:T(8,128)}, u32[]{:S(2)}, u32[]{:S(2)}) async-start(f32[8,64,768]{2,1,0:T(8,128)} %bitcast.266), calls=%async_computation.7 | async-start | bytes 3145728 | tf_op jit(solution)/shard_map/all_to_all | solution.py:248
  (9 other events, 14.7 us)
Sparse Core Ops, SparseCore 0:
  44.9 30.1 all-gather.14
  78.0 100.6 all-gather.8
  181.6 118.1 all-gather.16
  302.5 112.5 all-gather.10
  577.4 181.9 reduce-scatter.7
  762.5 74.1 all-gather.12
  867.2 57.3 reduce-scatter.11
  928.2 118.2 reduce-scatter.9
  1048.9 184.1 reduce-scatter.5
  1236.0 32.5 reduce-scatter.13
